TPU v7x, 256 devices: a whole 4x4x8 slice. The times are simulated.
256 devices in a mesh: band: 16 (over x_lo, z), slab: 16 (over y, x_hi, core).
Axes of the slice: x: 4 (x_hi: 2, x_lo: 2; x = x_hi * 2 + x_lo), y: 4, z: 8, core: 2. Of those that a mesh axis runs over, the one named last changes fastest.
Arguments:
- orbitals: float32 [256, 48, 2304], P('band', 'slab'), may hold values from -6 to 6
- partners: int32 [16, 2], replicated, may hold values from 0 to 15, as said below
- counts: int32 [16, 2], replicated, may hold values from 1 to 16
Outputs:
- forces: float32 [256, 48, 2304], P('band', 'slab')
- energy: float32 [], replicated
Inputs may be any that keep to these rules, and one draw needn't show every extreme that they name: `partners`: row g names two different band groups, neither of them g.
All inputs are finite; a program needn't handle non-finite values.
Results may differ from a plain program's by a relative error of at most 0.0001.
Values sent between devices are 32-bit elements; how exact they have to be, the bound alone decides.
A program may use at most 64 MiB of HBM per device.

v0:
```python
import functools
import math
import jax
import jax.numpy as jnp
from jax import lax
from jax.sharding import Mesh
from jax.sharding import PartitionSpec as P

NX = 48
NY = 48
NZ = 48
NZP = 96
BAND = ("band_0", "band_1")
SLAB = ("slab_0", "slab_1", "slab_2")
BAND_SLAB = ("band_0", "band_1", "slab_0", "slab_1", "slab_2")
slater_coeff = -((3.0 / math.pi) ** (1.0 / 3.0))
exchange_mix = 0.25
screening = 0.25
highest = lax.Precision.HIGHEST


def over_axes(value, axes):
    return functools.reduce(lax.psum, axes, value)


def dft_block(count_in, count_out, length, sign):
    row_iota = lax.broadcasted_iota(jnp.int32, (count_in, count_out), 0)
    col_iota = lax.broadcasted_iota(jnp.int32, (count_in, count_out), 1)
    phase_angle = 2.0 * math.pi / length * (row_iota * col_iota % length).astype(jnp.float32)
    cosine = jnp.cos(phase_angle)
    sine = jnp.sin(phase_angle)
    upper = jnp.stack([cosine, -sign * sine])
    lower = jnp.stack([sign * sine, cosine])
    return jnp.stack([upper, lower])


def wavenumber_sq(length):
    position = jnp.arange(length, dtype=jnp.int32)
    signed = jnp.where(position > length // 2, position - length, position).astype(jnp.float32)
    wave_number = 2.0 * math.pi / length * signed
    return wave_number * wave_number


def screened_potential(fields):
    spectrum = jnp.einsum(
        "coxyz,cdzk->doxyk", fields, dft_block(NZ, NZP, NZP, 1.0), precision=highest
    )
    spectrum = jnp.einsum(
        "coxyk,cdyq->doxqk", spectrum, dft_block(NY, NY, NY, 1.0), precision=highest
    )
    spectrum = jnp.einsum(
        "coxqk,cdxp->dopqk", spectrum, dft_block(NX, NX, NX, 1.0), precision=highest
    )
    total = (
        wavenumber_sq(NX)[:, None, None]
        + wavenumber_sq(NY)[None, :, None]
        + wavenumber_sq(NZP)[None, None, :]
    )
    kernel_table = 4.0 * math.pi / (NX * NY * NZP) / (total + screening * screening)
    spectrum = spectrum * kernel_table
    spectrum = jnp.einsum(
        "copqk,cdpx->doxqk", spectrum, dft_block(NX, NX, NX, -1.0), precision=highest
    )
    spectrum = jnp.einsum(
        "coxqk,cdqy->doxyk", spectrum, dft_block(NY, NY, NY, -1.0), precision=highest
    )
    return jnp.einsum(
        "coxyk,cdkz->doxyz", spectrum, dft_block(NZP, NZ, NZP, -1.0), precision=highest
    )


def pair_terms(own_orbs, visitors, active):
    per_device = own_orbs.shape[0]
    pair_density = own_orbs[None] * visitors * active[:, :, None, None]
    shaped = pair_density.reshape(2, per_device, NX, NY, NZ)
    fields = screened_potential(shaped).reshape(pair_density.shape)
    own_force = -exchange_mix * jnp.sum(fields * visitors, axis=0)
    partner_force = -exchange_mix * fields * own_orbs[None]
    energy_term = jnp.sum(pair_density * fields)
    return (own_force, partner_force, energy_term)


def request_rows(held_rows, partners, width):
    row_index = (partners[:, :, None] * width + jnp.arange(width, dtype=jnp.int32)).reshape(-1)
    return jnp.take(held_rows, row_index, axis=0)


def return_rows(pieces, partners, bands):
    flat = pieces.reshape(bands * 2, -1)
    targets = jnp.arange(bands, dtype=jnp.int32)[:, None]
    onehot = (partners.reshape(-1)[None, :] == targets).astype(jnp.float32)
    summed = jnp.dot(onehot, flat, precision=highest)
    width = pieces.shape[0] // (bands * 2)
    return summed.reshape((bands * width,) + pieces.shape[1:])


def body(orbitals, partners, counts):
    bands = lax.axis_size(BAND)
    slabs = lax.axis_size(SLAB)
    band_index = lax.axis_index(BAND)
    slab_index = lax.axis_index(SLAB)
    orb_group = orbitals.shape[0]
    per_device = orb_group // slabs
    total_orbs = orb_group * bands
    squares = jnp.sum(orbitals * orbitals, axis=0)
    density = 2.0 / total_orbs * over_axes(squares, BAND)
    local_pot = slater_coeff * jnp.cbrt(density)
    band_match = jnp.arange(bands, dtype=jnp.int32)[:, None] == band_index
    my_counts = jnp.sum(jnp.where(band_match, counts, 0), axis=0)
    local_rows = slab_index * per_device + jnp.arange(per_device, dtype=jnp.int32)
    active = (local_rows[None, :] < my_counts[:, None]).astype(jnp.float32)
    own_orbs = lax.all_to_all(orbitals, SLAB, split_axis=0, concat_axis=1, tiled=True)
    held_rows = lax.all_to_all(own_orbs, BAND, split_axis=1, concat_axis=0, tiled=True)
    wanted = request_rows(held_rows, partners, per_device)
    visitors = lax.all_to_all(wanted, BAND, split_axis=0, concat_axis=1, tiled=True)
    visitors = visitors.reshape((2, per_device) + own_orbs.shape[1:])
    own_force, partner_force, energy_term = pair_terms(own_orbs, visitors, active)
    outgoing = partner_force.reshape((2 * per_device,) + own_orbs.shape[1:])
    outgoing = lax.all_to_all(outgoing, BAND, split_axis=1, concat_axis=0, tiled=True)
    returned = lax.all_to_all(
        return_rows(outgoing, partners, bands), BAND, split_axis=0, concat_axis=1, tiled=True
    )
    exchange_force = lax.all_to_all(
        own_force + returned, SLAB, split_axis=1, concat_axis=0, tiled=True
    )
    energy_total = over_axes(energy_term, BAND_SLAB)
    energy = -energy_total / (2.0 * total_orbs * NX * NY * NZ)
    forces = local_pot[None] * orbitals + exchange_force
    return (forces, energy)


def solution(mesh):
    torus = Mesh(
        mesh.devices.reshape(2, 8, 4, 2, 2), ("band_0", "band_1", "slab_0", "slab_1", "slab_2")
    )
    in_specs = (P(BAND, SLAB, None), P(), P())
    out_specs = (P(BAND, SLAB, None), P())
    return jax.shard_map(body, mesh=torus, in_specs=in_specs, out_specs=out_specs, check_vma=False)
```

profile of v0, /device:TPU:1, one launch (start us, length us, event | category | flops | bytes accessed | tf_op | source)
XLA Modules:
  0.0 241.4 jit_solution(8340046165394980093)
XLA Ops:
  0.6 2.1 copy.93
  2.8 8.4 %all-to-all-start = ((f32[16,3,2304]{2,1,0:T(4,128)}), f32[16,3,2304]{2,1,0:T(4,128)S(1)}, u32[]{:S(2)}, u32[]{:S(2)}) async-start(f32[16,3,2304]{2,1,0:T(4,128)} %copy.93), calls=%async_computation | async-start | bytes 1179648 | tf_op jit(solution)/shard_map/all_to_all | solution.py:112
  11.2 0.8 copy.98
  11.9 0.1 reshape_broadcast_in_dim.6
  12.1 0.8 select_reduce_fusion
  12.9 0.1 broadcast_multiply_fusion.3
  13.0 0.1 broadcast_multiply_fusion.4
  13.1 9.9 %all-to-all-done = f32[16,3,2304]{2,1,0:T(4,128)S(1)} async-done(((f32[16,3,2304]{2,1,0:T(4,128)}), f32[16,3,2304]{2,1,0:T(4,128)S(1)}, u32[]{:S(2)}, u32[]{:S(2)}) %all-to-all-start) | async-done | bytes 442400 | tf_op jit(solution)/shard_map/all_to_all | solution.py:112
  23.1 1.4 all_to_all.72
  24.4 8.4 %all-to-all-start.1 = ((f32[1,48,2304]{2,0,1:T(1,128)}), f32[1,48,2304]{2,0,1:T(1,128)S(1)}, u32[]{:S(2)}, u32[]{:S(2)}) async-start(f32[1,48,2304]{2,0,1:T(1,128)} %all_to_all.72), calls=%async_computation.1 | async-start | bytes 884736 | tf_op jit(solution)/shard_map/all_to_all | solution.py:113
  32.9 0.1 broadcast_multiply_fusion.5
  33.0 0.1 fusion.59
  33.1 0.1 fusion.63
  33.3 0.1 fusion.67
  33.4 0.6 maximum_bitcast_fusion.10
  34.1 10.5 %all-to-all-done.1 = f32[1,48,2304]{2,0,1:T(1,128)S(1)} async-done(((f32[1,48,2304]{2,0,1:T(1,128)}), f32[1,48,2304]{2,0,1:T(1,128)S(1)}, u32[]{:S(2)}, u32[]{:S(2)}) %all-to-all-start.1) | async-done | bytes 442400 | tf_op jit(solution)/shard_map/all_to_all | solution.py:113
  44.5 1.0 reduce.3
  45.6 0.2 all_to_all.61
  45.8 1.3 gather_fusion
  47.0 1.3 broadcast_select_fusion
  48.4 5.8 %all-to-all-start.2 = ((f32[32,3,2304]{2,1,0:T(4,128)}), f32[32,3,2304]{2,1,0:T(4,128)S(1)}, u32[]{:S(2)}, u32[]{:S(2)}) async-start(f32[32,3,2304]{2,1,0:T(4,128)} %broadcast_select_fusion), calls=%async_computation.2 | async-start | bytes 2359296 | tf_op jit(solution)/shard_map/all_to_all | solution.py:115
  54.2 0.6 maximum_bitcast_fusion.8
  54.9 0.7 fusion.49
  55.7 1.4 add_divide_fusion
  57.1 0.8 mul.413
  57.9 1.4 copy.119
  59.3 0.1 broadcast_multiply_fusion.2
  59.5 1.0 mul.434
  60.4 21.4 %all-to-all-done.2 = f32[32,3,2304]{2,1,0:T(4,128)S(1)} async-done(((f32[32,3,2304]{2,1,0:T(4,128)}), f32[32,3,2304]{2,1,0:T(4,128)S(1)}, u32[]{:S(2)}, u32[]{:S(2)}) %all-to-all-start.2) | async-done | bytes 884768 | tf_op jit(solution)/shard_map/all_to_all | solution.py:115
  81.8 1.4 copy.189
  83.2 2.7 %reshape.398 = f32[2,48,48,48]{3,2,0,1:T(8,128)S(1)} reshape(f32[2,16,3,2304]{3,0,2,1:T(2,128)} %bitcast.149) | data formatting | bytes 1769472 | tf_op jit(solution)/shard_map/reshape | solution.py:116
  85.9 3.6 %reshape.402 = f32[2,1,48,48,48]{4,3,0,2,1:T(8,128)} reshape(f32[2,16,3,2304]{3,0,2,1:T(2,128)} %bitcast.150) | data formatting | bytes 1769472 | tf_op jit(solution)/shard_map/reshape | solution.py:116
  89.6 3.0 %fusion.19 = f32[2,48,48,96]{3,2,1,0:T(8,128)S(1)} fusion(f32[2,48,48,48]{3,2,0,1:T(8,128)S(1)} %reshape.398, f32[2]{0:T(128)S(1)} %compare_convert_fusion, f32[48,48,48]{2,1,0:T(8,128)S(1)} %mul.413, f32[1,2,48,96]{3,2,0,1:T(8,128)} %get-tuple-element.25, f32[1,2,48,96]{3,2,0,1:T(8,128)} %get-tuple-element.24), kind=kOutput, calls=%fused_computation.23 | convolution fusion | flops 510068736 | bytes 3170312 | tf_op jit(solution)/shard_map/coxyz,cdzk->doxyk/dot_general | solution.py:45
  92.7 2.2 fusion.22
  94.9 2.7 %bitcast_multiply_fusion = f32[2,48,48,96]{3,1,2,0:T(8,128)S(1)} fusion(f32[2,48,48,96]{3,2,1,0:T(8,128)S(1)} %fusion.22, f32[48,48,96]{2,0,1:T(8,128)S(1)} %copy-done, f32[1,2,48,48]{2,3,0,1:T(8,128)S(1)} %copy-done.5, f32[1,2,48,48]{2,3,0,1:T(8,128)S(1)} %copy-done.6), kind=kOutput, calls=%fused_computation.7 | convolution fusion | flops 510059520 | bytes 4460544 | tf_op jit(solution)/shard_map/coxqk,cdxp->dopqk/dot_general | solution.py:51
  97.7 2.2 fusion.27
  99.9 2.7 %fusion.30 = f32[2,48,48,96]{3,2,1,0:T(8,128)S(1)} fusion(f32[2,48,48,96]{3,1,2,0:T(8,128)S(1)} %fusion.27, f32[1,2,48,48]{2,3,1,0:T(8,128)S(1)} %copy-done.4, f32[1,2,48,48]{2,3,1,0:T(8,128)S(1)} %copy-done.3), kind=kOutput, calls=%fused_computation.26 | convolution fusion | flops 509617152 | bytes 3575808 | tf_op jit(solution)/shard_map/coxqk,cdqy->doxyk/dot_general | solution.py:64
  102.6 3.0 %copy.111 = f32[2,1,48,48,48]{3,4,2,0,1:T(8,128)} copy(f32[2,1,48,48,48]{4,3,0,2,1:T(8,128)} %reshape.402) | data formatting | bytes 1769472 | tf_op jit(solution)/shard_map/reshape | solution.py:116
  105.6 8.1 %multiply_reduce_fusion = (f32[]{:T(128)}, f32[48,48,48]{1,2,0:T(8,128)S(1)}, f32[2,1,48,48,48]{3,4,2,0,1:T(8,128)}) fusion(f32[2,1,48,48,48]{3,4,2,0,1:T(8,128)} %copy.111, f32[2]{0:T(128)S(1)} %compare_convert_fusion, f32[48,48,48]{1,2,0:T(8,128)} %copy.119, f32[2,48,48,96]{3,2,1,0:T(8,128)S(1)} %fusion.30, f32[1,2,96,48]{2,3,0,1:T(8,128)} %get-tuple-element.21, ...), kind=kOutput, calls=%fused_computation.19 | convolution fusion | flops 510842880 | bytes 4497420 | tf_op jit(solution)/shard_map/coxyk,cdkz->doxyz/dot_general | solution.py:67
  113.8 2.0 copy.113
  115.8 1.9 reshape.403
  117.7 1.4 broadcast_multiply_fusion.1
  119.1 0.7 copy.114
  119.8 28.6 %all_to_all.79 = f32[2,48,2304]{2,0,1:T(2,128)S(1)} all-to-all(f32[2,48,2304]{2,0,1:T(2,128)S(1)} %copy.114), channel_id=1, replica_groups=mesh['band_0'=2,'band_1'=8,'slab_0'=4,'slab_1'=2,'slab_2'=2] {'band_0','..., dimensions={1} | all-to-all | bytes 1769472 | tf_op jit(solution)/shard_map/all_to_all | solution.py:119
  148.4 0.3 copy.115
  148.7 0.5 fusion.38
  149.2 1.1 copy.117
  150.3 5.7 %all-to-all-start.4 = ((f32[16,3,2304]{2,1,0:T(4,128)}), f32[16,3,2304]{2,1,0:T(4,128)}, u32[]{:S(2)}, u32[]{:S(2)}) async-start(f32[16,3,2304]{2,1,0:T(4,128)} %copy.117), calls=%async_computation.4 | async-start | bytes 1179648 | tf_op jit(solution)/shard_map/all_to_all | solution.py:120
  156.1 0.1 multiply_reduce_fusion.2
  156.1 9.3 %all-reduce.1 = (f32[3,2304]{1,0:T(4,128)S(1)}, f32[]{:T(128)}) all-reduce(f32[3,2304]{1,0:T(4,128)S(1)} %multiply_reduce_fusion.2, f32[]{:T(128)} %get-tuple-element.10), channel_id=1, replica_groups=mesh['band_0'=2,'band_1'=8,'slab_0'=4,'slab_1'=2,'slab_2'=2] {'band_0'}, use_global_device_ids=true, to_apply=%region_1.0 | all-reduce | flops 6913 | bytes 55304 | tf_op jit(solution)/shard_map/psum | solution.py:23
  165.4 24.0 %all-reduce = (f32[3,2304]{1,0:T(4,128)}, f32[]{:T(128)}) all-reduce(f32[3,2304]{1,0:T(4,128)S(1)} %get-tuple-element.14, f32[]{:T(128)} %get-tuple-element.15), channel_id=1, replica_groups=mesh['band_0'=2,'band_1'=8,'slab_0'=4,'slab_1'=2,'slab_2'=2] {'band_1'}, use_global_device_ids=true, to_apply=%region_2.0 | all-reduce | flops 6913 | bytes 55304 | tf_op jit(solution)/shard_map/psum | solution.py:23
  189.4 7.1 %psum.53 = f32[]{:T(128)} all-reduce(f32[]{:T(128)} %get-tuple-element.13), channel_id=1, replica_groups=mesh['band_0'=2,'band_1'=8,'slab_0'=4,'slab_1'=2,'slab_2'=2] {'slab_0'}, use_global_device_ids=true, to_apply=%region_8.9 | all-reduce | flops 1 | bytes 8 | tf_op jit(solution)/shard_map/psum | solution.py:23
  196.5 5.9 %psum.54 = f32[]{:T(128)} all-reduce(f32[]{:T(128)} %psum.53), channel_id=1, replica_groups=mesh['band_0'=2,'band_1'=8,'slab_0'=4,'slab_1'=2,'slab_2'=2] {'slab_1'}, use_global_device_ids=true, to_apply=%region_9.10 | all-reduce | flops 1 | bytes 8 | tf_op jit(solution)/shard_map/psum | solution.py:23
  202.4 15.8 %psum.55 = f32[]{:T(128)} all-reduce(f32[]{:T(128)} %psum.54), channel_id=1, replica_groups=mesh['band_0'=2,'band_1'=8,'slab_0'=4,'slab_1'=2,'slab_2'=2] {'slab_2'}, use_global_device_ids=true, to_apply=%region_10.11 | all-reduce | flops 1 | bytes 8 | tf_op jit(solution)/shard_map/psum | solution.py:23
  218.3 0.4 copy.112
  218.7 0.5 mul.431
  219.8 1.3 all_to_all.69
  221.2 1.2 copy.118
  222.4 5.1 %all-to-all-start.5 = ((f32[1,48,2304]{2,0,1:T(1,128)}), f32[1,48,2304]{2,0,1:T(1,128)S(1)}, u32[]{:S(2)}, u32[]{:S(2)}) async-start(f32[1,48,2304]{2,0,1:T(1,128)} %copy.118), calls=%async_computation.5 | async-start | bytes 884736 | tf_op jit(solution)/shard_map/all_to_all | solution.py:123
  227.6 10.2 %all-to-all-done.5 = f32[1,48,2304]{2,0,1:T(1,128)S(1)} async-done(((f32[1,48,2304]{2,0,1:T(1,128)}), f32[1,48,2304]{2,0,1:T(1,128)S(1)}, u32[]{:S(2)}, u32[]{:S(2)}) %all-to-all-start.5) | async-done | bytes 442400 | tf_op jit(solution)/shard_map/all_to_all | solution.py:123
  237.8 1.0 reduce.4
  238.9 0.2 all_to_all.71
  239.1 0.4 multiply_add_fusion
  239.4 0.8 copy.121
  (29 shorter events, 0.4 us)
Async XLA Ops:
  2.8 20.3 %all-to-all-start = ((f32[16,3,2304]{2,1,0:T(4,128)}), f32[16,3,2304]{2,1,0:T(4,128)S(1)}, u32[]{:S(2)}, u32[]{:S(2)}) async-start(f32[16,3,2304]{2,1,0:T(4,128)} %copy.93), calls=%async_computation | async-start | bytes 1179648 | tf_op jit(solution)/shard_map/all_to_all | solution.py:112
  24.4 20.1 %all-to-all-start.1 = ((f32[1,48,2304]{2,0,1:T(1,128)}), f32[1,48,2304]{2,0,1:T(1,128)S(1)}, u32[]{:S(2)}, u32[]{:S(2)}) async-start(f32[1,48,2304]{2,0,1:T(1,128)} %all_to_all.72), calls=%async_computation.1 | async-start | bytes 884736 | tf_op jit(solution)/shard_map/all_to_all | solution.py:113
  48.4 33.5 %all-to-all-start.2 = ((f32[32,3,2304]{2,1,0:T(4,128)}), f32[32,3,2304]{2,1,0:T(4,128)S(1)}, u32[]{:S(2)}, u32[]{:S(2)}) async-start(f32[32,3,2304]{2,1,0:T(4,128)} %broadcast_select_fusion), calls=%async_computation.2 | async-start | bytes 2359296 | tf_op jit(solution)/shard_map/all_to_all | solution.py:115
  89.6 3.1 %copy-start.5 = (f32[1,2,48,48]{2,3,0,1:T(8,128)S(1)}, f32[1,2,48,48]{2,3,0,1:T(8,128)}, u32[]{:S(2)}) copy-start(f32[1,2,48,48]{2,3,0,1:T(8,128)} %get-tuple-element.17) | copy-start | bytes 55300
  89.6 3.1 %copy-start.6 = (f32[1,2,48,48]{2,3,0,1:T(8,128)S(1)}, f32[1,2,48,48]{2,3,0,1:T(8,128)}, u32[]{:S(2)}) copy-start(f32[1,2,48,48]{2,3,0,1:T(8,128)} %get-tuple-element.22) | copy-start | bytes 55300
  92.7 2.2 copy-start
  94.9 2.8 %copy-start.3 = (f32[1,2,48,48]{2,3,1,0:T(8,128)S(1)}, f32[1,2,48,48]{2,3,1,0:T(8,128)}, u32[]{:S(2)}) copy-start(f32[1,2,48,48]{2,3,1,0:T(8,128)} %get-tuple-element.16) | copy-start | bytes 55300
  94.9 2.8 %copy-start.4 = (f32[1,2,48,48]{2,3,1,0:T(8,128)S(1)}, f32[1,2,48,48]{2,3,1,0:T(8,128)}, u32[]{:S(2)}) copy-start(f32[1,2,48,48]{2,3,1,0:T(8,128)} %get-tuple-element.23) | copy-start | bytes 55300
  148.4 7.6 %copy-start.1 = (f32[16,3,2304]{2,0,1:T(8,128)S(1)}, f32[16,3,2304]{2,0,1:T(8,128)}, u32[]{:S(2)}) copy-start(f32[16,3,2304]{2,0,1:T(8,128)} %param.3) | copy-start | bytes 1327108
  150.3 69.5 %all-to-all-start.4 = ((f32[16,3,2304]{2,1,0:T(4,128)}), f32[16,3,2304]{2,1,0:T(4,128)}, u32[]{:S(2)}, u32[]{:S(2)}) async-start(f32[16,3,2304]{2,1,0:T(4,128)} %copy.117), calls=%async_computation.4 | async-start | bytes 1179648 | tf_op jit(solution)/shard_map/all_to_all | solution.py:120
  219.2 8.4 %copy-start.7 = (f32[3,2304]{1,0:T(4,128)S(1)}, f32[3,2304]{1,0:T(4,128)}, u32[]{:S(2)}) copy-start(f32[3,2304]{1,0:T(4,128)} %get-tuple-element.12) | copy-start | bytes 82948
  221.1 17.9 %copy-start.2 = (f32[16,3,2304]{2,0,1:T(8,128)S(1)}, f32[16,3,2304]{2,0,1:T(8,128)}, u32[]{:S(2)}) copy-start(f32[16,3,2304]{2,0,1:T(8,128)} %param.3) | copy-start | bytes 1327108
  222.4 15.4 %all-to-all-start.5 = ((f32[1,48,2304]{2,0,1:T(1,128)}), f32[1,48,2304]{2,0,1:T(1,128)S(1)}, u32[]{:S(2)}, u32[]{:S(2)}) async-start(f32[1,48,2304]{2,0,1:T(1,128)} %copy.118), calls=%async_computation.5 | async-start | bytes 884736 | tf_op jit(solution)/shard_map/all_to_all | solution.py:123
where the time goes:
time: 242 us; the launch traced here: 241 us
  blocking collectives  90.7 us (37%)
  waiting for transfers between devices  52 us (21%)
  starting transfers between devices  33.5 us (14%)
  local copies, waits for them, and re-layouts  30.4 us (13%)
  matrix products  21.5 us (9%)
  other arithmetic  10.6 us (4%)
  between operations  2.8 us (1%)
    psum x5, blocking collectives, over_axes(): return functools.reduce(lax.psum, axes, value)  62.1 us
    all_to_all x1, blocking collectives, body(): lax.all_to_all(outgoing, BAND, split_axis=1, concat_axis=0, tiled=True)  28.6 us
    all_to_all x1, waiting for transfers between devices, body(): lax.all_to_all(wanted, BAND, split_axis=0, concat_axis=1, tiled=True)  21.4 us
    all_to_all x1, waiting for transfers between devices, body(): lax.all_to_all(own_orbs, BAND, split_axis=1, concat_axis=0, tiled=True)  10.5 us
    all_to_all x1, waiting for transfers between devices, body(): lax.all_to_all(own_force + returned, SLAB, split_axis=1, concat_axis=0, t...  10.2 us
    all_to_all x1, waiting for transfers between devices, body(): lax.all_to_all(orbitals, SLAB, split_axis=0, concat_axis=1, tiled=True)  9.94 us
    reshape x3, local copies, waits for them, and re-layouts, body(): visitors = visitors.reshape((2, per_device) + own_orbs.shape[1:])  9.42 us
    all_to_all x1, starting transfers between devices, body(): lax.all_to_all(orbitals, SLAB, split_axis=0, concat_axis=1, tiled=True)  8.44 us
  transfers between devices with their start and end apart: 5, of which 4 were waited for; matrix products, arithmetic and copies ran while one was open for 4% of the time, Pallas kernels for 0%

commit v1 on v0

--- a/solution.py
+++ b/solution.py
@@ -110,7 +110,10 @@
     local_rows = slab_index * per_device + jnp.arange(per_device, dtype=jnp.int32)
     active = (local_rows[None, :] < my_counts[:, None]).astype(jnp.float32)
     own_orbs = lax.all_to_all(orbitals, SLAB, split_axis=0, concat_axis=1, tiled=True)
-    held_rows = lax.all_to_all(own_orbs, BAND, split_axis=1, concat_axis=0, tiled=True)
+    held_rows = jnp.concatenate(
+        lax.all_to_all(jnp.stack(jnp.split(own_orbs, lax.axis_size(BAND), axis=1)), BAND, 0, 0),
+        axis=0,
+    )
     wanted = request_rows(held_rows, partners, per_device)
     visitors = lax.all_to_all(wanted, BAND, split_axis=0, concat_axis=1, tiled=True)
     visitors = visitors.reshape((2, per_device) + own_orbs.shape[1:])

time: 242 us -> 242 us (level)
  no operation moved by 1% of the time
where the time goes in v1:
time: 242 us; the launch traced here: 241 us
  blocking collectives  90.7 us (37%)
  waiting for transfers between devices  52 us (21%)
  starting transfers between devices  33.4 us (14%)
  local copies, waits for them, and re-layouts  30.9 us (13%)
  matrix products  21.5 us (9%)
  other arithmetic  9.52 us (4%)
  between operations  2.88 us (1%)
    psum x5, blocking collectives, over_axes(): return functools.reduce(lax.psum, axes, value)  62.1 us
    all_to_all x1, blocking collectives, body(): lax.all_to_all(outgoing, BAND, split_axis=1, concat_axis=0, tiled=True)  28.6 us
    all_to_all x1, waiting for transfers between devices, body(): lax.all_to_all(wanted, BAND, split_axis=0, concat_axis=1, tiled=True)  21.4 us
    all_to_all x1, waiting for transfers between devices, body(): lax.all_to_all(jnp.stack(jnp.split(own_orbs, lax.axis_size(BAND), axis=1)...  10.5 us
    all_to_all x1, waiting for transfers between devices, body(): lax.all_to_all(own_force + returned, SLAB, split_axis=1, concat_axis=0, t...  10.2 us
    all_to_all x1, waiting for transfers between devices, body(): lax.all_to_all(orbitals, SLAB, split_axis=0, concat_axis=1, tiled=True)  9.94 us
    reshape x3, local copies, waits for them, and re-layouts, body(): visitors = visitors.reshape((2, per_device) + own_orbs.shape[1:])  9.42 us
    all_to_all x1, starting transfers between devices, body(): lax.all_to_all(orbitals, SLAB, split_axis=0, concat_axis=1, tiled=True)  8.44 us
  transfers between devices with their start and end apart: 5, of which 4 were waited for; matrix products, arithmetic and copies ran while one was open for 4% of the time, Pallas kernels for 0%

profile of v1, /device:TPU:1, one launch (start us, length us, event | category | flops | bytes accessed | tf_op | source)
XLA Modules:
  0.0 241.0 jit_solution(6755862884331229820)
XLA Ops:
  0.6 2.1 copy.122
  2.8 8.4 %all-to-all-start = ((f32[16,3,2304]{2,1,0:T(4,128)}), f32[16,3,2304]{2,1,0:T(4,128)S(1)}, u32[]{:S(2)}, u32[]{:S(2)}) async-start(f32[16,3,2304]{2,1,0:T(4,128)} %copy.122), calls=%async_computation | async-start | bytes 1179648 | tf_op jit(solution)/shard_map/all_to_all | solution.py:112
  11.2 0.8 copy.127
  11.9 0.1 reshape_broadcast_in_dim.6
  12.1 0.8 select_reduce_fusion
  12.9 0.1 broadcast_multiply_fusion.3
  13.0 0.1 broadcast_multiply_fusion.4
  13.1 9.9 %all-to-all-done = f32[16,3,2304]{2,1,0:T(4,128)S(1)} async-done(((f32[16,3,2304]{2,1,0:T(4,128)}), f32[16,3,2304]{2,1,0:T(4,128)S(1)}, u32[]{:S(2)}, u32[]{:S(2)}) %all-to-all-start) | async-done | bytes 442400 | tf_op jit(solution)/shard_map/all_to_all | solution.py:112
  23.1 0.2 all_to_all.53
  23.6 1.2 copy.128
  24.9 8.4 %all-to-all-start.1 = ((f32[16,1,3,2304]{3,1,2,0:T(1,128)}), f32[16,1,3,2304]{3,1,2,0:T(1,128)S(1)}, u32[]{:S(2)}, u32[]{:S(2)}) async-start(f32[16,1,3,2304]{3,1,2,0:T(1,128)} %copy.128), calls=%async_computation.1 | async-start | bytes 884736 | tf_op jit(solution)/shard_map/all_to_all | solution.py:114
  33.3 0.1 broadcast_multiply_fusion.5
  33.5 0.1 fusion.75
  33.6 0.1 fusion.79
  33.7 0.1 fusion.83
  33.8 0.6 maximum_bitcast_fusion.10
  34.5 10.5 %all-to-all-done.1 = f32[16,1,3,2304]{3,1,2,0:T(1,128)S(1)} async-done(((f32[16,1,3,2304]{3,1,2,0:T(1,128)}), f32[16,1,3,2304]{3,1,2,0:T(1,128)S(1)}, u32[]{:S(2)}, u32[]{:S(2)}) %all-to-all-start.1) | async-done | bytes 442400 | tf_op jit(solution)/shard_map/all_to_all | solution.py:114
  45.0 0.3 copy.131
  45.3 1.3 gather_fusion
  46.6 1.3 broadcast_select_fusion
  47.9 5.8 %all-to-all-start.2 = ((f32[32,3,2304]{2,1,0:T(4,128)}), f32[32,3,2304]{2,1,0:T(4,128)S(1)}, u32[]{:S(2)}, u32[]{:S(2)}) async-start(f32[32,3,2304]{2,1,0:T(4,128)} %broadcast_select_fusion), calls=%async_computation.2 | async-start | bytes 2359296 | tf_op jit(solution)/shard_map/all_to_all | solution.py:118
  53.8 0.6 maximum_bitcast_fusion.8
  54.4 0.7 fusion.49
  55.2 1.4 add_divide_fusion
  56.6 0.8 mul.413
  57.4 1.4 copy.150
  58.9 0.1 broadcast_multiply_fusion.2
  59.0 1.0 mul.434
  60.0 21.4 %all-to-all-done.2 = f32[32,3,2304]{2,1,0:T(4,128)S(1)} async-done(((f32[32,3,2304]{2,1,0:T(4,128)}), f32[32,3,2304]{2,1,0:T(4,128)S(1)}, u32[]{:S(2)}, u32[]{:S(2)}) %all-to-all-start.2) | async-done | bytes 884768 | tf_op jit(solution)/shard_map/all_to_all | solution.py:118
  81.4 1.4 copy.220
  82.8 2.7 %reshape.399 = f32[2,48,48,48]{3,2,0,1:T(8,128)S(1)} reshape(f32[2,16,3,2304]{3,0,2,1:T(2,128)} %bitcast.216) | data formatting | bytes 1769472 | tf_op jit(solution)/shard_map/reshape | solution.py:119
  85.5 3.6 %reshape.403 = f32[2,1,48,48,48]{4,3,0,2,1:T(8,128)} reshape(f32[2,16,3,2304]{3,0,2,1:T(2,128)} %bitcast.217) | data formatting | bytes 1769472 | tf_op jit(solution)/shard_map/reshape | solution.py:119
  89.1 3.0 %fusion.19 = f32[2,48,48,96]{3,2,1,0:T(8,128)S(1)} fusion(f32[2,48,48,48]{3,2,0,1:T(8,128)S(1)} %reshape.399, f32[2]{0:T(128)S(1)} %compare_convert_fusion, f32[48,48,48]{2,1,0:T(8,128)S(1)} %mul.413, f32[1,2,48,96]{3,2,0,1:T(8,128)} %get-tuple-element.27, f32[1,2,48,96]{3,2,0,1:T(8,128)} %get-tuple-element.26), kind=kOutput, calls=%fused_computation.23 | convolution fusion | flops 510068736 | bytes 3170312 | tf_op jit(solution)/shard_map/coxyz,cdzk->doxyk/dot_general | solution.py:45
  92.2 2.2 fusion.22
  94.5 2.7 %bitcast_multiply_fusion = f32[2,48,48,96]{3,1,2,0:T(8,128)S(1)} fusion(f32[2,48,48,96]{3,2,1,0:T(8,128)S(1)} %fusion.22, f32[48,48,96]{2,0,1:T(8,128)S(1)} %copy-done, f32[1,2,48,48]{2,3,0,1:T(8,128)S(1)} %copy-done.5, f32[1,2,48,48]{2,3,0,1:T(8,128)S(1)} %copy-done.6), kind=kOutput, calls=%fused_computation.7 | convolution fusion | flops 510059520 | bytes 4460544 | tf_op jit(solution)/shard_map/coxqk,cdxp->dopqk/dot_general | solution.py:51
  97.2 2.2 fusion.27
  99.4 2.7 %fusion.30 = f32[2,48,48,96]{3,2,1,0:T(8,128)S(1)} fusion(f32[2,48,48,96]{3,1,2,0:T(8,128)S(1)} %fusion.27, f32[1,2,48,48]{2,3,1,0:T(8,128)S(1)} %copy-done.4, f32[1,2,48,48]{2,3,1,0:T(8,128)S(1)} %copy-done.3), kind=kOutput, calls=%fused_computation.26 | convolution fusion | flops 509617152 | bytes 3575808 | tf_op jit(solution)/shard_map/coxqk,cdqy->doxyk/dot_general | solution.py:64
  102.1 3.0 %copy.142 = f32[2,1,48,48,48]{3,4,2,0,1:T(8,128)} copy(f32[2,1,48,48,48]{4,3,0,2,1:T(8,128)} %reshape.403) | data formatting | bytes 1769472 | tf_op jit(solution)/shard_map/reshape | solution.py:119
  105.2 8.1 %multiply_reduce_fusion = (f32[]{:T(128)}, f32[48,48,48]{1,2,0:T(8,128)S(1)}, f32[2,1,48,48,48]{3,4,2,0,1:T(8,128)}) fusion(f32[2,1,48,48,48]{3,4,2,0,1:T(8,128)} %copy.142, f32[2]{0:T(128)S(1)} %compare_convert_fusion, f32[48,48,48]{1,2,0:T(8,128)} %copy.150, f32[2,48,48,96]{3,2,1,0:T(8,128)S(1)} %fusion.30, f32[1,2,96,48]{2,3,0,1:T(8,128)} %get-tuple-element.23, ...), kind=kOutput, calls=%fused_computation.19 | convolution fusion | flops 510842880 | bytes 4497420 | tf_op jit(solution)/shard_map/coxyk,cdkz->doxyz/dot_general | solution.py:67
  113.3 2.0 copy.144
  115.3 1.9 reshape.404
  117.3 1.4 broadcast_multiply_fusion.1
  118.6 0.7 copy.145
  119.3 28.6 %all_to_all.71 = f32[2,48,2304]{2,0,1:T(2,128)S(1)} all-to-all(f32[2,48,2304]{2,0,1:T(2,128)S(1)} %copy.145), channel_id=1, replica_groups=mesh['band_0'=2,'band_1'=8,'slab_0'=4,'slab_1'=2,'slab_2'=2] {'band_0','..., dimensions={1} | all-to-all | bytes 1769472 | tf_op jit(solution)/shard_map/all_to_all | solution.py:122
  147.9 0.3 copy.146
  148.3 0.5 fusion.38
  148.7 1.1 copy.148
  149.8 5.7 %all-to-all-start.4 = ((f32[16,3,2304]{2,1,0:T(4,128)}), f32[16,3,2304]{2,1,0:T(4,128)}, u32[]{:S(2)}, u32[]{:S(2)}) async-start(f32[16,3,2304]{2,1,0:T(4,128)} %copy.148), calls=%async_computation.4 | async-start | bytes 1179648 | tf_op jit(solution)/shard_map/all_to_all | solution.py:123
  155.6 0.1 multiply_reduce_fusion.2
  155.7 9.3 %all-reduce.1 = (f32[3,2304]{1,0:T(4,128)S(1)}, f32[]{:T(128)}) all-reduce(f32[3,2304]{1,0:T(4,128)S(1)} %multiply_reduce_fusion.2, f32[]{:T(128)} %get-tuple-element.12), channel_id=1, replica_groups=mesh['band_0'=2,'band_1'=8,'slab_0'=4,'slab_1'=2,'slab_2'=2] {'band_0'}, use_global_device_ids=true, to_apply=%region_1.0 | all-reduce | flops 6913 | bytes 55304 | tf_op jit(solution)/shard_map/psum | solution.py:23
  165.0 24.0 %all-reduce = (f32[3,2304]{1,0:T(4,128)}, f32[]{:T(128)}) all-reduce(f32[3,2304]{1,0:T(4,128)S(1)} %get-tuple-element.16, f32[]{:T(128)} %get-tuple-element.17), channel_id=1, replica_groups=mesh['band_0'=2,'band_1'=8,'slab_0'=4,'slab_1'=2,'slab_2'=2] {'band_1'}, use_global_device_ids=true, to_apply=%region_2.0 | all-reduce | flops 6913 | bytes 55304 | tf_op jit(solution)/shard_map/psum | solution.py:23
  188.9 7.1 %psum.53 = f32[]{:T(128)} all-reduce(f32[]{:T(128)} %get-tuple-element.15), channel_id=1, replica_groups=mesh['band_0'=2,'band_1'=8,'slab_0'=4,'slab_1'=2,'slab_2'=2] {'slab_0'}, use_global_device_ids=true, to_apply=%region_8.9 | all-reduce | flops 1 | bytes 8 | tf_op jit(solution)/shard_map/psum | solution.py:23
  196.1 5.9 %psum.54 = f32[]{:T(128)} all-reduce(f32[]{:T(128)} %psum.53), channel_id=1, replica_groups=mesh['band_0'=2,'band_1'=8,'slab_0'=4,'slab_1'=2,'slab_2'=2] {'slab_1'}, use_global_device_ids=true, to_apply=%region_9.10 | all-reduce | flops 1 | bytes 8 | tf_op jit(solution)/shard_map/psum | solution.py:23
  202.0 15.8 %psum.55 = f32[]{:T(128)} all-reduce(f32[]{:T(128)} %psum.54), channel_id=1, replica_groups=mesh['band_0'=2,'band_1'=8,'slab_0'=4,'slab_1'=2,'slab_2'=2] {'slab_2'}, use_global_device_ids=true, to_apply=%region_10.11 | all-reduce | flops 1 | bytes 8 | tf_op jit(solution)/shard_map/psum | solution.py:23
  217.9 0.4 copy.143
  218.2 0.5 mul.431
  219.4 1.3 all_to_all.62
  220.8 1.2 copy.149
  222.0 5.1 %all-to-all-start.5 = ((f32[1,48,2304]{2,0,1:T(1,128)}), f32[1,48,2304]{2,0,1:T(1,128)S(1)}, u32[]{:S(2)}, u32[]{:S(2)}) async-start(f32[1,48,2304]{2,0,1:T(1,128)} %copy.149), calls=%async_computation.5 | async-start | bytes 884736 | tf_op jit(solution)/shard_map/all_to_all | solution.py:126
  227.2 10.2 %all-to-all-done.5 = f32[1,48,2304]{2,0,1:T(1,128)S(1)} async-done(((f32[1,48,2304]{2,0,1:T(1,128)}), f32[1,48,2304]{2,0,1:T(1,128)S(1)}, u32[]{:S(2)}, u32[]{:S(2)}) %all-to-all-start.5) | async-done | bytes 442400 | tf_op jit(solution)/shard_map/all_to_all | solution.py:126
  237.4 1.0 reduce.3
  238.4 0.2 all_to_all.64
  238.6 0.4 multiply_add_fusion
  239.0 0.8 copy.152
  (46 shorter events, 0.7 us)
Async XLA Ops:
  2.8 20.3 %all-to-all-start = ((f32[16,3,2304]{2,1,0:T(4,128)}), f32[16,3,2304]{2,1,0:T(4,128)S(1)}, u32[]{:S(2)}, u32[]{:S(2)}) async-start(f32[16,3,2304]{2,1,0:T(4,128)} %copy.122), calls=%async_computation | async-start | bytes 1179648 | tf_op jit(solution)/shard_map/all_to_all | solution.py:112
  24.9 20.1 %all-to-all-start.1 = ((f32[16,1,3,2304]{3,1,2,0:T(1,128)}), f32[16,1,3,2304]{3,1,2,0:T(1,128)S(1)}, u32[]{:S(2)}, u32[]{:S(2)}) async-start(f32[16,1,3,2304]{3,1,2,0:T(1,128)} %copy.128), calls=%async_computation.1 | async-start | bytes 884736 | tf_op jit(solution)/shard_map/all_to_all | solution.py:114
  47.9 33.5 %all-to-all-start.2 = ((f32[32,3,2304]{2,1,0:T(4,128)}), f32[32,3,2304]{2,1,0:T(4,128)S(1)}, u32[]{:S(2)}, u32[]{:S(2)}) async-start(f32[32,3,2304]{2,1,0:T(4,128)} %broadcast_select_fusion), calls=%async_computation.2 | async-start | bytes 2359296 | tf_op jit(solution)/shard_map/all_to_all | solution.py:118
  89.1 3.1 %copy-start.5 = (f32[1,2,48,48]{2,3,0,1:T(8,128)S(1)}, f32[1,2,48,48]{2,3,0,1:T(8,128)}, u32[]{:S(2)}) copy-start(f32[1,2,48,48]{2,3,0,1:T(8,128)} %get-tuple-element.19) | copy-start | bytes 55300
  89.1 3.1 %copy-start.6 = (f32[1,2,48,48]{2,3,0,1:T(8,128)S(1)}, f32[1,2,48,48]{2,3,0,1:T(8,128)}, u32[]{:S(2)}) copy-start(f32[1,2,48,48]{2,3,0,1:T(8,128)} %get-tuple-element.24) | copy-start | bytes 55300
  92.2 2.2 copy-start
  94.4 2.8 %copy-start.3 = (f32[1,2,48,48]{2,3,1,0:T(8,128)S(1)}, f32[1,2,48,48]{2,3,1,0:T(8,128)}, u32[]{:S(2)}) copy-start(f32[1,2,48,48]{2,3,1,0:T(8,128)} %get-tuple-element.18) | copy-start | bytes 55300
  94.5 2.8 %copy-start.4 = (f32[1,2,48,48]{2,3,1,0:T(8,128)S(1)}, f32[1,2,48,48]{2,3,1,0:T(8,128)}, u32[]{:S(2)}) copy-start(f32[1,2,48,48]{2,3,1,0:T(8,128)} %get-tuple-element.25) | copy-start | bytes 55300
  147.9 7.7 %copy-start.1 = (f32[16,3,2304]{2,0,1:T(8,128)S(1)}, f32[16,3,2304]{2,0,1:T(8,128)}, u32[]{:S(2)}) copy-start(f32[16,3,2304]{2,0,1:T(8,128)} %param.3) | copy-start | bytes 1327108
  149.8 69.6 %all-to-all-start.4 = ((f32[16,3,2304]{2,1,0:T(4,128)}), f32[16,3,2304]{2,1,0:T(4,128)}, u32[]{:S(2)}, u32[]{:S(2)}) async-start(f32[16,3,2304]{2,1,0:T(4,128)} %copy.148), calls=%async_computation.4 | async-start | bytes 1179648 | tf_op jit(solution)/shard_map/all_to_all | solution.py:123
  218.7 8.3 %copy-start.7 = (f32[3,2304]{1,0:T(4,128)S(1)}, f32[3,2304]{1,0:T(4,128)}, u32[]{:S(2)}) copy-start(f32[3,2304]{1,0:T(4,128)} %get-tuple-element.14) | copy-start | bytes 82948
  220.7 17.9 %copy-start.2 = (f32[16,3,2304]{2,0,1:T(8,128)S(1)}, f32[16,3,2304]{2,0,1:T(8,128)}, u32[]{:S(2)}) copy-start(f32[16,3,2304]{2,0,1:T(8,128)} %param.3) | copy-start | bytes 1327108
  222.0 15.4 %all-to-all-start.5 = ((f32[1,48,2304]{2,0,1:T(1,128)}), f32[1,48,2304]{2,0,1:T(1,128)S(1)}, u32[]{:S(2)}, u32[]{:S(2)}) async-start(f32[1,48,2304]{2,0,1:T(1,128)} %copy.149), calls=%async_computation.5 | async-start | bytes 884736 | tf_op jit(solution)/shard_map/all_to_all | solution.py:126
